TPU v7x, 512 devices: a whole 4x8x8 slice. The times are simulated.
512 devices in a mesh: section: 4 (over y_lo), row: 16 (over z, core), col: 8 (over y_hi, x).
Axes of the slice: x: 4, y: 8 (y_hi: 2, y_lo: 4; y = y_hi * 4 + y_lo), z: 8, core: 2. Of those that a mesh axis runs over, the one named last changes fastest.
Arguments:
- section_input: bfloat16 [4, 2, 128, 128, 128], P('section', None, 'row', 'col'), may hold values from -6 to 6
- first_pre: bfloat16 [4, 2, 128, 128, 128], P('section', None, 'row', 'col'), may hold values from -6 to 6
- second_pre: bfloat16 [4, 2, 128, 128, 128], P('section', None, 'row', 'col'), may hold values from -6 to 6
- out_grad: bfloat16 [2, 128, 128, 128], P(None, 'row', 'col'), may hold values from -6 to 6
- kernels: bfloat16 [4, 2, 3, 3, 128, 128], P('section'), may hold values from -0.1875 to 0.1875
- bn_scale: float32 [4, 2, 128], P('section'), may hold values from 0.5 to 2
- bn_shift: float32 [4, 2, 128], P('section'), may hold values from -3 to 3
Outputs:
- input_grad: bfloat16 [4, 2, 128, 128, 128], P('section', None, 'row', 'col')
- filter_grad: float32 [4, 2, 3, 3, 128, 128], P('section')
All inputs are finite; a program needn't handle non-finite values.
Results may differ from a plain program's by a relative error of at most 0.013.
Values may be sent and summed in bfloat16 or wider, within the bound.
No kernel may reach another device: no remote copies, remote signals or barrier semaphores. Data moves between devices by JAX's collectives and lax.ppermute only.
A program may use at most 64 MiB of HBM per device.

v0:
```python
import jax
import jax.numpy as jnp
from jax import lax
from jax.sharding import Mesh
from jax.sharding import PartitionSpec as P

ROW = ("row_0", "row_1")
COL = ("col_0", "col_1")
NEAR = ("row_1", "col_1")
FAR = ("row_0", "col_0")


def with_halo(cells, axis, dim, width):
    count = lax.axis_size(axis)
    size = cells.shape[dim]
    head = lax.slice_in_dim(cells, 0, width, axis=dim)
    tail = lax.slice_in_dim(cells, size - width, size, axis=dim)
    before = lax.ppermute(tail, axis, [(i, i + 1) for i in range(count - 1)])
    after = lax.ppermute(head, axis, [(i + 1, i) for i in range(count - 1)])
    return jnp.concatenate([before, cells, after], axis=dim)


def crop(field, cut):
    if cut == 0:
        return field
    return field[:, cut:-cut, cut:-cut]


def correlate(padded, kernel):
    return lax.conv_general_dilated(
        padded,
        kernel,
        (1, 1),
        "VALID",
        dimension_numbers=("NHWC", "HWIO", "NHWC"),
        preferred_element_type=jnp.float32,
    )


def flip_kernel(kernel):
    return jnp.transpose(jnp.flip(kernel, (0, 1)), (0, 1, 3, 2))


def kernel_grad(cells, padded):
    rows_here, cols_here = (cells.shape[1], cells.shape[2])
    windows = jnp.stack(
        [
            padded[:, 2 - i : 2 - i + rows_here, 2 - j : 2 - j + cols_here]
            for i in range(3)
            for j in range(3)
        ]
    )
    return jnp.einsum("mhwc,kmhwd->kcd", cells, windows, preferred_element_type=jnp.float32)


def sum_of_blocks(blocks, axes):
    parts = lax.all_to_all(blocks, axes, 0, 0, tiled=True)
    return jnp.sum(parts.astype(jnp.float32), axis=0)


def copies(block, axes):
    count = lax.axis_size(axes)
    return lax.all_to_all(
        jnp.broadcast_to(block[None], (count, *block.shape)), axes, 0, 0, tiled=True
    )


def total_of(x, factor):
    near, stack = (lax.axis_size(NEAR), lax.axis_size("row_0"))
    width = x.shape[-1]
    lines = x.astype(jnp.bfloat16).reshape(near, -1, width)
    part = sum_of_blocks(lines, NEAR).astype(jnp.bfloat16).reshape(stack, 1, -1, width)
    twice = jnp.broadcast_to(part, (stack, lax.axis_size("col_0"), *part.shape[2:]))
    own = sum_of_blocks(twice.reshape(-1, *part.shape[2:]), FAR)
    own = (own * factor).astype(jnp.bfloat16)
    part = lax.all_gather(own, "row_0", axis=0, tiled=True)
    return copies(part, NEAR).reshape(x.shape).astype(jnp.float32)


def on_device(section_input, first_pre, second_pre, out_grad, kernels, bn_scale, bn_shift):
    section_index = lax.axis_index("section")
    sections = lax.axis_size("section")
    last = section_index == sections - 1
    micros, rows_here, cols_here, width = out_grad.shape
    inputs = section_input[0]
    kernel = kernels[0]
    scales = bn_scale[0]
    shifts = bn_shift[0]
    first_norm = scales[0] * first_pre[0].astype(jnp.float32) + shifts[0]
    first_act = jnp.maximum(first_norm, 0.0).astype(jnp.bfloat16)
    second_norm = scales[1] * second_pre[0].astype(jnp.float32) + shifts[1]
    alive = second_norm + inputs.astype(jnp.float32) > 0
    one = jnp.ones((), jnp.bfloat16)
    zero = jnp.zeros((), jnp.bfloat16)
    passed = jnp.where(alive, jnp.where(last, out_grad, one), zero)
    first_on = jnp.where(first_norm > 0, one, zero)
    depth = 2 * sections
    masks = jnp.stack([passed, first_on])
    masks = with_halo(masks, COL, 3, depth)
    masks = with_halo(masks, ROW, 2, depth)
    passed, first_on = (masks[0], masks[1])
    flip_first = flip_kernel(kernel[0])
    flip_second = flip_kernel(kernel[1])

    def unit(incoming, reach):
        masked = crop(passed, depth - reach - 2)
        if incoming is not None:
            masked = masked * incoming
        masked = masked.astype(jnp.float32)
        second_grad = (scales[1] * masked).astype(jnp.bfloat16)
        act_grad = correlate(second_grad, flip_second)
        on = crop(first_on, depth - reach - 1).astype(jnp.float32)
        first_grad = (scales[0] * (act_grad * on)).astype(jnp.bfloat16)
        result = crop(masked, 2) + correlate(first_grad, flip_first)
        return (result.astype(jnp.bfloat16), first_grad, second_grad)

    received = None
    own_incoming = jnp.where(last, one, zero)
    for step in range(sections - 1):
        reach = 2 * (sections - 1 - step)
        result, _, _ = unit(received, reach)
        received = lax.ppermute(result, "section", [(sections - 1 - step, sections - 2 - step)])
        own_incoming = own_incoming + crop(received, reach - 2)
    input_grad, first_grad, second_grad = unit(own_incoming, 0)
    partial = jnp.stack(
        [kernel_grad(inputs, first_grad), kernel_grad(first_act, crop(second_grad, 1))]
    )
    pixels = micros * rows_here * lax.axis_size(ROW) * cols_here * lax.axis_size(COL)
    factor = 1.0 / jnp.sqrt(jnp.float32(pixels))
    total = total_of(partial, factor).reshape(2, 3, 3, width, width)
    return (input_grad[None], total[None])


def solution(mesh):
    split = Mesh(
        mesh.devices.reshape(mesh.shape["section"], 8, 2, 2, 4),
        ("section", "row_0", "row_1", "col_0", "col_1"),
    )
    in_specs = (
        P("section", None, ROW, COL, None),
        P("section", None, ROW, COL, None),
        P("section", None, ROW, COL, None),
        P(None, ROW, COL, None),
        P("section", None, None, None, None, None),
        P("section", None, None),
        P("section", None, None),
    )
    out_specs = (P("section", None, ROW, COL, None), P("section", None, None, None, None, None))
    return jax.shard_map(
        on_device, mesh=split, in_specs=in_specs, out_specs=out_specs, check_vma=False
    )
```

profile of v0, /device:TPU:1, one launch (start us, length us, event | category | flops | bytes accessed | tf_op | source)
XLA Modules:
  0.0 150.6 jit_solution(10677023709551831681)
XLA Ops:
  0.6 0.8 slice_bitcast_fusion.26
  1.4 0.9 fusion.103
  2.3 1.0 fusion.104
  3.3 3.9 %collective-permute-start = (bf16[2,2,8,8,128]{4,3,1,2,0:T(8,128)(2,1)S(1)}, bf16[2,2,8,8,128]{4,3,1,2,0:T(8,128)(2,1)S(1)}, u32[]{:S(2)}, u32[]{:S(2)}) collective-permute-start(bf16[2,2,8,8,128]{4,3,1,2,0:T(8,128)(2,1)S(1)} %get-tuple-element.19), channel_id=1, source_target_pairs={{0,1},{1,2},{2,3},{3,4},{4,5},{5,6},{6,7},{8,9},{9,10},{10,11},{11... | collective-permute-start | bytes 196616 | tf_op jit(solution)/shard_map/ppermute | solution.py:18
  7.2 1.3 collective-permute-start.1
  8.5 3.7 %collective-permute-done.1 = bf16[2,2,8,8,128]{4,3,1,2,0:T(8,128)(2,1)S(1)} collective-permute-done((bf16[2,2,8,8,128]{4,3,1,2,0:T(8,128)(2,1)S(1)}, bf16[2,2,8,8,128]{4,3,1,2,0:T(8,128)(2,1)S(1)}, u32[]{:S(2)}, u32[]{:S(2)}) %collective-permute-start.1) | collective-permute-done | bytes 65568 | tf_op jit(solution)/shard_map/ppermute | solution.py:19
  12.3 7.3 %collective-permute-start.3 = (bf16[2,2,8,32,128]{4,3,1,2,0:T(8,128)(2,1)S(1)}, bf16[2,2,8,32,128]{4,3,1,2,0:T(8,128)(2,1)S(1)}, u32[]{:S(2)}, u32[]{:S(2)}) collective-permute-start(bf16[2,2,8,32,128]{4,3,1,2,0:T(8,128)(2,1)S(1)} %pad_maximum_fusion.2), channel_id=1, source_target_pairs={{8,0},{16,8},{24,16},{32,24},{40,32},{48,40},{56,48},{64,56},{72,6... | collective-permute-start | bytes 786440 | tf_op jit(solution)/shard_map/ppermute | solution.py:19
  19.5 1.9 %collective-permute-start.2 = (bf16[2,2,8,32,128]{4,3,1,2,0:T(8,128)(2,1)S(1)}, bf16[2,2,8,32,128]{4,3,1,2,0:T(8,128)(2,1)S(1)}, u32[]{:S(2)}, u32[]{:S(2)}) collective-permute-start(bf16[2,2,8,32,128]{4,3,1,2,0:T(8,128)(2,1)S(1)} %pad_maximum_fusion.2), channel_id=1, source_target_pairs={{0,8},{8,16},{16,24},{24,32},{32,40},{40,48},{48,56},{56,64},{64,7... | collective-permute-start | bytes 786440 | tf_op jit(solution)/shard_map/ppermute | solution.py:18
  21.4 0.8 collective-permute-done.3
  22.3 2.4 %collective-permute-done.2 = bf16[2,2,8,32,128]{4,3,1,2,0:T(8,128)(2,1)S(1)} collective-permute-done((bf16[2,2,8,32,128]{4,3,1,2,0:T(8,128)(2,1)S(1)}, bf16[2,2,8,32,128]{4,3,1,2,0:T(8,128)(2,1)S(1)}, u32[]{:S(2)}, u32[]{:S(2)}) %collective-permute-start.2) | collective-permute-done | bytes 262176 | tf_op jit(solution)/shard_map/ppermute | solution.py:18
  24.8 0.1 multiply_convert_fusion
  24.9 0.2 slice_bitcast_fusion.4
  25.3 0.9 copy-done.2
  26.2 1.0 convolution_select_fusion
  27.2 0.3 copy.193
  27.5 0.2 fusion.42
  27.9 0.5 copy-done.9
  28.4 0.9 convolution_select_fusion.1
  29.3 0.3 copy.196
  29.6 0.1 fusion.12
  29.7 0.7 collective-permute-start.4
  30.4 0.2 fusion.47
  30.7 0.3 copy-done.8
  31.0 0.9 convolution_select_fusion.2
  31.9 0.2 copy.199
  32.2 0.1 fusion.51
  32.5 0.4 copy-done.7
  32.8 0.8 convolution_select_fusion.3
  33.6 0.3 copy.202
  34.0 0.1 fusion.48
  34.1 0.2 fusion.41
  34.2 0.7 collective-permute-start.5
  35.2 0.6 convolution_select_fusion.4
  35.8 0.1 copy.206
  35.9 0.1 fusion.88
  36.1 0.1 copy.236
  36.2 0.1 pad.8.clone
  36.4 0.2 fusion.63
  36.7 0.5 convolution_select_fusion.5
  37.2 0.2 copy.210
  37.4 0.1 reshape.98
  37.6 1.3 collective-permute-start.6
  38.9 15.0 %collective-permute-done.6 = bf16[2,12,20,128]{3,2,0,1:T(8,128)(2,1)S(1)} collective-permute-done((bf16[2,12,20,128]{3,2,0,1:T(8,128)(2,1)S(1)}, bf16[2,12,20,128]{3,2,0,1:T(8,128)(2,1)S(1)}, u32[]{:S(2)}, u32[]{:S(2)}) %collective-permute-start.6) | collective-permute-done | bytes 122912 | tf_op jit(solution)/shard_map/ppermute | solution.py:122
  54.0 0.2 multiply_convert_fusion.3
  54.3 0.1 pad.10.clone
  54.5 0.2 fusion.67
  54.7 0.5 convolution_select_fusion.6
  55.2 0.1 copy.213
  55.3 0.1 reshape.100
  55.8 0.4 copy-done.1
  56.1 0.3 fusion.4
  56.7 0.3 fusion.3
  57.1 23.5 %all_to_all.15 = bf16[8,288,128]{2,1,0:T(8,128)(2,1)S(1)} all-to-all(bf16[8,288,128]{2,1,0:T(8,128)(2,1)S(1)} %bitcast.307), channel_id=1, replica_groups=mesh['section'=4,'row_0'=8,'row_1'=2,'col_0'=2,'col_1'=4] {'row_1','col_1'}, dimensions={0} | all-to-all | bytes 1179648 | tf_op jit(solution)/shard_map/all_to_all | solution.py:57
  80.7 0.7 broadcast_in_dim.38
  81.4 15.1 %all-to-all-start.1 = ((bf16[16,36,128]{2,1,0:T(8,128)(2,1)}), bf16[16,36,128]{2,1,0:T(8,128)(2,1)S(1)}, u32[]{:S(2)}, u32[]{:S(2)}) async-start(bf16[16,36,128]{2,1,0:T(8,128)(2,1)} %bitcast.91), calls=%async_computation.1 | async-start | bytes 327680 | tf_op jit(solution)/shard_map/all_to_all | solution.py:57
  96.7 12.0 %all-to-all-done.1 = bf16[16,36,128]{2,1,0:T(8,128)(2,1)S(1)} async-done(((bf16[16,36,128]{2,1,0:T(8,128)(2,1)}), bf16[16,36,128]{2,1,0:T(8,128)(2,1)S(1)}, u32[]{:S(2)}, u32[]{:S(2)}) %all-to-all-start.1) | async-done | bytes 147488 | tf_op jit(solution)/shard_map/all_to_all | solution.py:57
  108.8 18.5 %all-gather = bf16[8,36,128]{2,1,0:T(8,128)(2,1)S(1)} all-gather(bf16[1,36,128]{2,1,0:T(8,128)(2,1)S(1)} %fusion.133), channel_id=1, replica_groups=mesh['section'=4,'row_0'=8,'row_1'=2,'col_0'=2,'col_1'=4] {'row_0'}, dimensions={0}, use_global_device_ids=true | all-gather | bytes 82944 | tf_op jit(solution)/shard_map/all_gather | solution.py:76
  127.3 0.9 broadcast_in_dim.39
  128.2 11.2 %all-to-all-start.2 = ((bf16[8,288,128]{2,1,0:T(8,128)(2,1)}), bf16[8,288,128]{2,1,0:T(8,128)(2,1)S(1)}, u32[]{:S(2)}, u32[]{:S(2)}) async-start(bf16[8,288,128]{2,1,0:T(8,128)(2,1)} %broadcast_in_dim.39), calls=%async_computation.2 | async-start | bytes 1179648 | tf_op jit(solution)/shard_map/all_to_all | solution.py:63
  139.4 0.2 fusion.75
  139.6 0.4 convolution_select_fusion.7
  140.1 0.6 copy.228
  140.7 8.7 %all-to-all-done.2 = bf16[8,288,128]{2,1,0:T(8,128)(2,1)S(1)} async-done(((bf16[8,288,128]{2,1,0:T(8,128)(2,1)}), bf16[8,288,128]{2,1,0:T(8,128)(2,1)S(1)}, u32[]{:S(2)}, u32[]{:S(2)}) %all-to-all-start.2) | async-done | bytes 589856 | tf_op jit(solution)/shard_map/all_to_all | solution.py:63
  149.4 1.1 convert.17
  (76 shorter events, 2.5 us)
Async XLA Ops:
  3.3 5.3 %collective-permute-start = (bf16[2,2,8,8,128]{4,3,1,2,0:T(8,128)(2,1)S(1)}, bf16[2,2,8,8,128]{4,3,1,2,0:T(8,128)(2,1)S(1)}, u32[]{:S(2)}, u32[]{:S(2)}) collective-permute-start(bf16[2,2,8,8,128]{4,3,1,2,0:T(8,128)(2,1)S(1)} %get-tuple-element.19), channel_id=1, source_target_pairs={{0,1},{1,2},{2,3},{3,4},{4,5},{5,6},{6,7},{8,9},{9,10},{10,11},{11... | collective-permute-start | bytes 196616 | tf_op jit(solution)/shard_map/ppermute | solution.py:18
  7.2 5.0 %collective-permute-start.1 = (bf16[2,2,8,8,128]{4,3,1,2,0:T(8,128)(2,1)S(1)}, bf16[2,2,8,8,128]{4,3,1,2,0:T(8,128)(2,1)S(1)}, u32[]{:S(2)}, u32[]{:S(2)}) collective-permute-start(bf16[2,2,8,8,128]{4,3,1,2,0:T(8,128)(2,1)S(1)} %get-tuple-element.20), channel_id=1, source_target_pairs={{1,0},{2,1},{3,2},{4,3},{5,4},{6,5},{7,6},{9,8},{10,9},{11,10},{12... | collective-permute-start | bytes 196616 | tf_op jit(solution)/shard_map/ppermute | solution.py:19
  12.3 10.0 %collective-permute-start.3 = (bf16[2,2,8,32,128]{4,3,1,2,0:T(8,128)(2,1)S(1)}, bf16[2,2,8,32,128]{4,3,1,2,0:T(8,128)(2,1)S(1)}, u32[]{:S(2)}, u32[]{:S(2)}) collective-permute-start(bf16[2,2,8,32,128]{4,3,1,2,0:T(8,128)(2,1)S(1)} %pad_maximum_fusion.2), channel_id=1, source_target_pairs={{8,0},{16,8},{24,16},{32,24},{40,32},{48,40},{56,48},{64,56},{72,6... | collective-permute-start | bytes 786440 | tf_op jit(solution)/shard_map/ppermute | solution.py:19
  19.5 5.2 %collective-permute-start.2 = (bf16[2,2,8,32,128]{4,3,1,2,0:T(8,128)(2,1)S(1)}, bf16[2,2,8,32,128]{4,3,1,2,0:T(8,128)(2,1)S(1)}, u32[]{:S(2)}, u32[]{:S(2)}) collective-permute-start(bf16[2,2,8,32,128]{4,3,1,2,0:T(8,128)(2,1)S(1)} %pad_maximum_fusion.2), channel_id=1, source_target_pairs={{0,8},{8,16},{16,24},{24,32},{32,40},{40,48},{48,56},{56,64},{64,7... | collective-permute-start | bytes 786440 | tf_op jit(solution)/shard_map/ppermute | solution.py:18
  25.1 1.1 copy-start.2
  25.2 1.1 copy-start.10
  27.7 0.7 copy-start.9
  29.7 0.7 collective-permute-start.4
  30.4 0.7 copy-start.8
  32.2 0.7 copy-start.7
  34.1 1.1 copy-start.6
  34.2 0.7 collective-permute-start.5
  35.9 0.8 copy-start.5
  37.6 16.4 %collective-permute-start.6 = (bf16[2,12,20,128]{3,2,0,1:T(8,128)(2,1)S(1)}, bf16[2,12,20,128]{3,2,0,1:T(8,128)(2,1)S(1)}, u32[]{:S(2)}, u32[]{:S(2)}) collective-permute-start(bf16[2,12,20,128]{3,2,0,1:T(8,128)(2,1)S(1)} %fusion.53), channel_id=1, source_target_pairs={{128,0},{129,1},{130,2},{131,3},{132,4},{133,5},{134,6},{135,7},{1... | collective-permute-start | bytes 368648 | tf_op jit(solution)/shard_map/ppermute | solution.py:122
  38.9 15.7 %copy-start.4 = (pred[16,3]{0,1:T(4,128)(4,1)S(1)}, pred[16,3]{0,1:T(4,128)(4,1)}, u32[]{:S(2)}) copy-start(pred[16,3]{0,1:T(4,128)(4,1)} %constant.62) | copy-start | bytes 148
  55.3 0.8 copy-start.1
  55.7 1.1 copy-start
  81.4 27.3 %all-to-all-start.1 = ((bf16[16,36,128]{2,1,0:T(8,128)(2,1)}), bf16[16,36,128]{2,1,0:T(8,128)(2,1)S(1)}, u32[]{:S(2)}, u32[]{:S(2)}) async-start(bf16[16,36,128]{2,1,0:T(8,128)(2,1)} %bitcast.91), calls=%async_computation.1 | async-start | bytes 327680 | tf_op jit(solution)/shard_map/all_to_all | solution.py:57
  127.3 12.3 %copy-start.3 = (pred[16,3]{0,1:T(4,128)(4,1)S(1)}, pred[16,3]{0,1:T(4,128)(4,1)}, u32[]{:S(2)}) copy-start(pred[16,3]{0,1:T(4,128)(4,1)} %constant.61) | copy-start | bytes 148
  128.2 21.2 %all-to-all-start.2 = ((bf16[8,288,128]{2,1,0:T(8,128)(2,1)}), bf16[8,288,128]{2,1,0:T(8,128)(2,1)S(1)}, u32[]{:S(2)}, u32[]{:S(2)}) async-start(bf16[8,288,128]{2,1,0:T(8,128)(2,1)} %broadcast_in_dim.39), calls=%async_computation.2 | async-start | bytes 1179648 | tf_op jit(solution)/shard_map/all_to_all | solution.py:63
where the time goes:
time: 151 us
  starting transfers between devices  43.3 us (29%)
  waiting for transfers between devices  42.7 us (28%)
  blocking collectives  42 us (28%)
  local copies, waits for them, and re-layouts  9.26 us (6%)
  matrix products  6.13 us (4%)
  other arithmetic  5.69 us (4%)
    all_to_all x1, blocking collectives, sum_of_blocks(): parts = lax.all_to_all(blocks, axes, 0, 0, tiled=True)  23.5 us
    all_gather x1, blocking collectives, total_of(): part = lax.all_gather(own, 'row_0', axis=0, tiled=True)  18.5 us
    all_to_all x1, starting transfers between devices, sum_of_blocks(): parts = lax.all_to_all(blocks, axes, 0, 0, tiled=True)  15.1 us
    ppermute x3, waiting for transfers between devices, on_device(): lax.ppermute(result, 'section', [(sections - 1 - step, sections - 2 - ste...  15 us
    all_to_all x1, waiting for transfers between devices, sum_of_blocks(): parts = lax.all_to_all(blocks, axes, 0, 0, tiled=True)  12 us
    all_to_all x1, starting transfers between devices, copies(): lax.all_to_all(jnp.broadcast_to(block[None], (count, *block.shape)), axes...  11.2 us
    all_to_all x1, waiting for transfers between devices, copies(): lax.all_to_all(jnp.broadcast_to(block[None], (count, *block.shape)), axes...  8.7 us
    ppermute x2, starting transfers between devices, with_halo(): after = lax.ppermute(head, axis, [(i + 1, i) for i in range(count - 1)])  8.55 us
  transfers between devices with their start and end apart: 9, of which 6 were waited for; matrix products, arithmetic and copies ran while one was open for 1% of the time, Pallas kernels for 0%

commit v1 on v0

--- a/solution.py
+++ b/solution.py
@@ -3,11 +3,19 @@
 from jax import lax
 from jax.sharding import Mesh
 from jax.sharding import PartitionSpec as P
+from jax.lax import all_to_all, axis_size
 
 ROW = ("row_0", "row_1")
 COL = ("col_0", "col_1")
 NEAR = ("row_1", "col_1")
 FAR = ("row_0", "col_0")
+
+
+def point_stages_all(incoming_x, in_dim):
+    current_value = jnp.stack([incoming_x] * axis_size("row_0"))
+    small = all_to_all(current_value, "row_0", 0, 0)
+    a_now = jnp.concatenate(small, axis=in_dim)
+    return a_now
 
 
 def with_halo(cells, axis, dim, width):
@@ -73,7 +81,7 @@
     twice = jnp.broadcast_to(part, (stack, lax.axis_size("col_0"), *part.shape[2:]))
     own = sum_of_blocks(twice.reshape(-1, *part.shape[2:]), FAR)
     own = (own * factor).astype(jnp.bfloat16)
-    part = lax.all_gather(own, "row_0", axis=0, tiled=True)
+    part = point_stages_all(own, 0)
     return copies(part, NEAR).reshape(x.shape).astype(jnp.float32)
 
 

time: 151 us -> 138 us (0.914)
  starting transfers between devices: 43.3 us -> 26.6 us
  blocking collectives: 42 us -> 50.6 us
  waiting for transfers between devices: 42.7 us -> 37.8 us
    all_to_all x1 -> x2, blocking collectives: 23.5 us -> 50.6 us  [sum_of_blocks(): parts = lax.all_to_all(blocks, axes, 0, 0, tiled=True)]
    all_gather x1 -> x0, blocking collectives: 18.5 us -> none  [total_of(): part = lax.all_gather(own, 'row_0', axis=0, tiled=True)]
    all_to_all x1, starting transfers between devices: 15.1 us -> 3.36 us  [point_stages_all(): small = all_to_all(current_value, 'row_0', 0, 0)]
    all_to_all x1, starting transfers between devices: 11.2 us -> 6.21 us  [copies(): lax.all_to_all(jnp.broadcast_to(block[None], (count, *block.shape)), axes...]
    all_to_all x1, waiting for transfers between devices: 12 us -> 7.07 us  [point_stages_all(): small = all_to_all(current_value, 'row_0', 0, 0)]
    unnamed x43 -> x42, local copies, waits for them, and re-layouts: 3.88 us -> 3.86 us
where the time goes in v1:
time: 138 us
  blocking collectives  50.6 us (37%)
  waiting for transfers between devices  37.8 us (27%)
  starting transfers between devices  26.6 us (19%)
  local copies, waits for them, and re-layouts  9.25 us (7%)
  matrix products  6.12 us (4%)
  other arithmetic  5.69 us (4%)
  between operations  1.46 us (1%)
    all_to_all x2, blocking collectives, sum_of_blocks(): parts = lax.all_to_all(blocks, axes, 0, 0, tiled=True)  50.6 us
    ppermute x3, waiting for transfers between devices, on_device(): lax.ppermute(result, 'section', [(sections - 1 - step, sections - 2 - ste...  15 us
    all_to_all x1, waiting for transfers between devices, copies(): lax.all_to_all(jnp.broadcast_to(block[None], (count, *block.shape)), axes...  8.7 us
    ppermute x2, starting transfers between devices, with_halo(): after = lax.ppermute(head, axis, [(i + 1, i) for i in range(count - 1)])  8.55 us
    all_to_all x1, waiting for transfers between devices, point_stages_all(): small = all_to_all(current_value, 'row_0', 0, 0)  7.07 us
    all_to_all x1, starting transfers between devices, copies(): lax.all_to_all(jnp.broadcast_to(block[None], (count, *block.shape)), axes...  6.21 us
    ppermute x2, starting transfers between devices, with_halo(): before = lax.ppermute(tail, axis, [(i, i + 1) for i in range(count - 1)])  5.86 us
    conv_general_dilated x8, matrix products, correlate(): lax.conv_general_dilated(padded, kernel, (1, 1), 'VALID', dimension_numbe...  5.53 us
  transfers between devices with their start and end apart: 9, of which 6 were waited for; matrix products, arithmetic and copies ran while one was open for 1% of the time, Pallas kernels for 0%

profile of v1, /device:TPU:1, one launch (start us, length us, event | category | flops | bytes accessed | tf_op | source)
XLA Modules:
  0.0 137.6 jit_solution(5787637013592487347)
XLA Ops:
  0.6 0.8 slice_bitcast_fusion.26
  1.4 0.9 fusion.103
  2.3 1.0 fusion.104
  3.3 3.9 %collective-permute-start = (bf16[2,2,8,8,128]{4,3,1,2,0:T(8,128)(2,1)S(1)}, bf16[2,2,8,8,128]{4,3,1,2,0:T(8,128)(2,1)S(1)}, u32[]{:S(2)}, u32[]{:S(2)}) collective-permute-start(bf16[2,2,8,8,128]{4,3,1,2,0:T(8,128)(2,1)S(1)} %get-tuple-element.17), channel_id=1, source_target_pairs={{0,1},{1,2},{2,3},{3,4},{4,5},{5,6},{6,7},{8,9},{9,10},{10,11},{11... | collective-permute-start | bytes 196616 | tf_op jit(solution)/shard_map/ppermute | solution.py:26
  7.2 1.3 collective-permute-start.1
  8.5 3.7 %collective-permute-done.1 = bf16[2,2,8,8,128]{4,3,1,2,0:T(8,128)(2,1)S(1)} collective-permute-done((bf16[2,2,8,8,128]{4,3,1,2,0:T(8,128)(2,1)S(1)}, bf16[2,2,8,8,128]{4,3,1,2,0:T(8,128)(2,1)S(1)}, u32[]{:S(2)}, u32[]{:S(2)}) %collective-permute-start.1) | collective-permute-done | bytes 65568 | tf_op jit(solution)/shard_map/ppermute | solution.py:27
  12.3 7.3 %collective-permute-start.3 = (bf16[2,2,8,32,128]{4,3,1,2,0:T(8,128)(2,1)S(1)}, bf16[2,2,8,32,128]{4,3,1,2,0:T(8,128)(2,1)S(1)}, u32[]{:S(2)}, u32[]{:S(2)}) collective-permute-start(bf16[2,2,8,32,128]{4,3,1,2,0:T(8,128)(2,1)S(1)} %pad_maximum_fusion.2), channel_id=1, source_target_pairs={{8,0},{16,8},{24,16},{32,24},{40,32},{48,40},{56,48},{64,56},{72,6... | collective-permute-start | bytes 786440 | tf_op jit(solution)/shard_map/ppermute | solution.py:27
  19.5 1.9 %collective-permute-start.2 = (bf16[2,2,8,32,128]{4,3,1,2,0:T(8,128)(2,1)S(1)}, bf16[2,2,8,32,128]{4,3,1,2,0:T(8,128)(2,1)S(1)}, u32[]{:S(2)}, u32[]{:S(2)}) collective-permute-start(bf16[2,2,8,32,128]{4,3,1,2,0:T(8,128)(2,1)S(1)} %pad_maximum_fusion.2), channel_id=1, source_target_pairs={{0,8},{8,16},{16,24},{24,32},{32,40},{40,48},{48,56},{56,64},{64,7... | collective-permute-start | bytes 786440 | tf_op jit(solution)/shard_map/ppermute | solution.py:26
  21.4 0.8 collective-permute-done.3
  22.3 2.4 %collective-permute-done.2 = bf16[2,2,8,32,128]{4,3,1,2,0:T(8,128)(2,1)S(1)} collective-permute-done((bf16[2,2,8,32,128]{4,3,1,2,0:T(8,128)(2,1)S(1)}, bf16[2,2,8,32,128]{4,3,1,2,0:T(8,128)(2,1)S(1)}, u32[]{:S(2)}, u32[]{:S(2)}) %collective-permute-start.2) | collective-permute-done | bytes 262176 | tf_op jit(solution)/shard_map/ppermute | solution.py:26
  24.8 0.1 multiply_convert_fusion
  24.9 0.2 slice_bitcast_fusion.4
  25.3 0.9 copy-done.2
  26.2 1.0 convolution_select_fusion
  27.2 0.3 copy.152
  27.5 0.2 fusion.42
  27.9 0.5 copy-done.9
  28.4 0.9 convolution_select_fusion.1
  29.3 0.3 copy.155
  29.6 0.1 fusion.12
  29.7 0.7 collective-permute-start.4
  30.4 0.2 fusion.47
  30.7 0.3 copy-done.8
  31.0 0.9 convolution_select_fusion.2
  31.9 0.2 copy.158
  32.2 0.1 fusion.51
  32.5 0.4 copy-done.7
  32.8 0.8 convolution_select_fusion.3
  33.6 0.3 copy.161
  34.0 0.1 fusion.48
  34.1 0.2 fusion.41
  34.2 0.7 collective-permute-start.5
  35.2 0.6 convolution_select_fusion.4
  35.8 0.1 copy.165
  35.9 0.1 fusion.88
  36.1 0.1 copy.195
  36.2 0.1 pad.8.clone
  36.4 0.2 fusion.63
  36.7 0.5 convolution_select_fusion.5
  37.2 0.2 copy.169
  37.4 0.1 reshape.100
  37.6 1.3 collective-permute-start.6
  38.9 15.0 %collective-permute-done.6 = bf16[2,12,20,128]{3,2,0,1:T(8,128)(2,1)S(1)} collective-permute-done((bf16[2,12,20,128]{3,2,0,1:T(8,128)(2,1)S(1)}, bf16[2,12,20,128]{3,2,0,1:T(8,128)(2,1)S(1)}, u32[]{:S(2)}, u32[]{:S(2)}) %collective-permute-start.6) | collective-permute-done | bytes 122912 | tf_op jit(solution)/shard_map/ppermute | solution.py:130
  54.0 0.2 multiply_convert_fusion.3
  54.3 0.1 pad.10.clone
  54.5 0.2 fusion.67
  54.7 0.5 convolution_select_fusion.6
  55.2 0.1 copy.172
  55.3 0.1 reshape.102
  55.8 0.4 copy-done.1
  56.1 0.3 fusion.4
  56.7 0.3 fusion.3
  57.1 23.5 %all_to_all.20 = bf16[8,288,128]{2,1,0:T(8,128)(2,1)S(1)} all-to-all(bf16[8,288,128]{2,1,0:T(8,128)(2,1)S(1)} %bitcast.305), channel_id=1, replica_groups=mesh['section'=4,'row_0'=8,'row_1'=2,'col_0'=2,'col_1'=4] {'row_1','col_1'}, dimensions={0} | all-to-all | bytes 1179648 | tf_op jit(solution)/shard_map/all_to_all | solution.py:65
  80.7 27.1 %all_to_all.21 = bf16[16,36,128]{2,1,0:T(8,128)(2,1)S(1)} all-to-all(bf16[16,36,128]{2,1,0:T(8,128)(2,1)S(1)} %bitcast.321), channel_id=1, replica_groups=mesh['section'=4,'row_0'=8,'row_1'=2,'col_0'=2,'col_1'=4] {'row_0','col_0'}, dimensions={0} | all-to-all | bytes 294912 | tf_op jit(solution)/shard_map/all_to_all | solution.py:65
  107.9 0.6 stack.115
  108.6 3.4 %all-to-all-start.2 = ((bf16[8,36,128]{2,1,0:T(8,128)(2,1)}), bf16[8,36,128]{2,1,0:T(8,128)(2,1)S(1)}, u32[]{:S(2)}, u32[]{:S(2)}) async-start(bf16[8,36,128]{2,1,0:T(8,128)(2,1)} %stack.115), calls=%async_computation.2 | async-start | bytes 163840 | tf_op jit(solution)/shard_map/all_to_all | solution.py:16
  112.2 7.1 %all-to-all-done.2 = bf16[8,36,128]{2,1,0:T(8,128)(2,1)S(1)} async-done(((bf16[8,36,128]{2,1,0:T(8,128)(2,1)}), bf16[8,36,128]{2,1,0:T(8,128)(2,1)S(1)}, u32[]{:S(2)}, u32[]{:S(2)}) %all-to-all-start.2) | async-done | bytes 73760 | tf_op jit(solution)/shard_map/all_to_all | solution.py:16
  119.3 0.9 broadcast_in_dim.41
  120.2 6.2 %all-to-all-start.3 = ((bf16[8,288,128]{2,1,0:T(8,128)(2,1)}), bf16[8,288,128]{2,1,0:T(8,128)(2,1)S(1)}, u32[]{:S(2)}, u32[]{:S(2)}) async-start(bf16[8,288,128]{2,1,0:T(8,128)(2,1)} %broadcast_in_dim.41), calls=%async_computation.3 | async-start | bytes 1179648 | tf_op jit(solution)/shard_map/all_to_all | solution.py:71
  126.4 0.2 fusion.75
  126.6 0.4 convolution_select_fusion.7
  127.1 0.6 copy.187
  127.7 8.7 %all-to-all-done.3 = bf16[8,288,128]{2,1,0:T(8,128)(2,1)S(1)} async-done(((bf16[8,288,128]{2,1,0:T(8,128)(2,1)}), bf16[8,288,128]{2,1,0:T(8,128)(2,1)S(1)}, u32[]{:S(2)}, u32[]{:S(2)}) %all-to-all-start.3) | async-done | bytes 589856 | tf_op jit(solution)/shard_map/all_to_all | solution.py:71
  136.4 1.1 convert.17
  (77 shorter events, 2.5 us)
Async XLA Ops:
  3.3 5.3 %collective-permute-start = (bf16[2,2,8,8,128]{4,3,1,2,0:T(8,128)(2,1)S(1)}, bf16[2,2,8,8,128]{4,3,1,2,0:T(8,128)(2,1)S(1)}, u32[]{:S(2)}, u32[]{:S(2)}) collective-permute-start(bf16[2,2,8,8,128]{4,3,1,2,0:T(8,128)(2,1)S(1)} %get-tuple-element.17), channel_id=1, source_target_pairs={{0,1},{1,2},{2,3},{3,4},{4,5},{5,6},{6,7},{8,9},{9,10},{10,11},{11... | collective-permute-start | bytes 196616 | tf_op jit(solution)/shard_map/ppermute | solution.py:26
  7.2 5.0 %collective-permute-start.1 = (bf16[2,2,8,8,128]{4,3,1,2,0:T(8,128)(2,1)S(1)}, bf16[2,2,8,8,128]{4,3,1,2,0:T(8,128)(2,1)S(1)}, u32[]{:S(2)}, u32[]{:S(2)}) collective-permute-start(bf16[2,2,8,8,128]{4,3,1,2,0:T(8,128)(2,1)S(1)} %get-tuple-element.18), channel_id=1, source_target_pairs={{1,0},{2,1},{3,2},{4,3},{5,4},{6,5},{7,6},{9,8},{10,9},{11,10},{12... | collective-permute-start | bytes 196616 | tf_op jit(solution)/shard_map/ppermute | solution.py:27
  12.3 10.0 %collective-permute-start.3 = (bf16[2,2,8,32,128]{4,3,1,2,0:T(8,128)(2,1)S(1)}, bf16[2,2,8,32,128]{4,3,1,2,0:T(8,128)(2,1)S(1)}, u32[]{:S(2)}, u32[]{:S(2)}) collective-permute-start(bf16[2,2,8,32,128]{4,3,1,2,0:T(8,128)(2,1)S(1)} %pad_maximum_fusion.2), channel_id=1, source_target_pairs={{8,0},{16,8},{24,16},{32,24},{40,32},{48,40},{56,48},{64,56},{72,6... | collective-permute-start | bytes 786440 | tf_op jit(solution)/shard_map/ppermute | solution.py:27
  19.5 5.2 %collective-permute-start.2 = (bf16[2,2,8,32,128]{4,3,1,2,0:T(8,128)(2,1)S(1)}, bf16[2,2,8,32,128]{4,3,1,2,0:T(8,128)(2,1)S(1)}, u32[]{:S(2)}, u32[]{:S(2)}) collective-permute-start(bf16[2,2,8,32,128]{4,3,1,2,0:T(8,128)(2,1)S(1)} %pad_maximum_fusion.2), channel_id=1, source_target_pairs={{0,8},{8,16},{16,24},{24,32},{32,40},{40,48},{48,56},{56,64},{64,7... | collective-permute-start | bytes 786440 | tf_op jit(solution)/shard_map/ppermute | solution.py:26
  25.1 1.1 copy-start.2
  25.2 1.1 copy-start.10
  27.7 0.7 copy-start.9
  29.7 0.7 collective-permute-start.4
  30.4 0.7 copy-start.8
  32.2 0.7 copy-start.7
  34.1 1.1 copy-start.6
  34.2 0.7 collective-permute-start.5
  35.9 0.8 copy-start.5
  37.6 16.4 %collective-permute-start.6 = (bf16[2,12,20,128]{3,2,0,1:T(8,128)(2,1)S(1)}, bf16[2,12,20,128]{3,2,0,1:T(8,128)(2,1)S(1)}, u32[]{:S(2)}, u32[]{:S(2)}) collective-permute-start(bf16[2,12,20,128]{3,2,0,1:T(8,128)(2,1)S(1)} %fusion.53), channel_id=1, source_target_pairs={{128,0},{129,1},{130,2},{131,3},{132,4},{133,5},{134,6},{135,7},{1... | collective-permute-start | bytes 368648 | tf_op jit(solution)/shard_map/ppermute | solution.py:130
  38.9 15.7 %copy-start.4 = (pred[16,3]{0,1:T(4,128)(4,1)S(1)}, pred[16,3]{0,1:T(4,128)(4,1)}, u32[]{:S(2)}) copy-start(pred[16,3]{0,1:T(4,128)(4,1)} %constant.62) | copy-start | bytes 148
  55.3 0.8 copy-start.1
  55.7 1.1 copy-start
  108.6 10.7 %all-to-all-start.2 = ((bf16[8,36,128]{2,1,0:T(8,128)(2,1)}), bf16[8,36,128]{2,1,0:T(8,128)(2,1)S(1)}, u32[]{:S(2)}, u32[]{:S(2)}) async-start(bf16[8,36,128]{2,1,0:T(8,128)(2,1)} %stack.115), calls=%async_computation.2 | async-start | bytes 163840 | tf_op jit(solution)/shard_map/all_to_all | solution.py:16
  112.2 14.4 %copy-start.3 = (pred[16,3]{0,1:T(4,128)(4,1)S(1)}, pred[16,3]{0,1:T(4,128)(4,1)}, u32[]{:S(2)}) copy-start(pred[16,3]{0,1:T(4,128)(4,1)} %constant.61) | copy-start | bytes 148
  120.2 16.3 %all-to-all-start.3 = ((bf16[8,288,128]{2,1,0:T(8,128)(2,1)}), bf16[8,288,128]{2,1,0:T(8,128)(2,1)S(1)}, u32[]{:S(2)}, u32[]{:S(2)}) async-start(bf16[8,288,128]{2,1,0:T(8,128)(2,1)} %broadcast_in_dim.41), calls=%async_computation.3 | async-start | bytes 1179648 | tf_op jit(solution)/shard_map/all_to_all | solution.py:71
